TPU v7x, 32 devices: a whole 2x2x4 slice. The times are simulated.
32 devices in a mesh: tm: 8 (over y, x, core), space: 4 (over z).
Axes of the slice: x: 2, y: 2, z: 4, core: 2. Of those that a mesh axis runs over, the one named last changes fastest.
Arguments:
- speed: float32 [8, 16, 128], P('space'), may hold values from 0.5 to 1.5
- forcing: float32 [32, 8, 16, 128], P('tm', 'space'), may hold values from -1.8 to 1.8
- guess: float32 [8, 4, 8, 16, 128], P('tm', None, 'space'), may hold values from -8 to 8
- basis: float32 [8, 64, 4, 8, 16, 128], P('tm', None, None, 'space'), may hold values from -1 to 1, as said below
Outputs:
- states: float32 [32, 4, 8, 16, 128], P('tm', None, 'space')
- coords: float32 [8, 64], P('tm')
Inputs may be any that keep to these rules, and one draw needn't show every extreme that they name: The columns of each basis[k] are linearly independent.
All inputs are finite; a program needn't handle non-finite values.
Results may differ from a plain program's by a relative error of at most 0.00018.
Values sent between devices are 32-bit elements; how exact they have to be, the bound alone decides.
A program may use at most 128 MiB of HBM per device.

v0:
```python
import jax
import jax.numpy as jnp
from jax import lax
from jax.experimental import pallas as pl
from jax.experimental.pallas import tpu as pltpu
from jax.sharding import PartitionSpec as P

DT = 0.045
GROUP = 4
MESH = pl.DeviceIdType.MESH


def phi(state, speed_sq, h):
    p, vx, vy, vz = state
    nx, ny = p.shape[1], p.shape[2]
    row = lax.broadcasted_iota(jnp.int32, p.shape, 1)
    lane = lax.broadcasted_iota(jnp.int32, p.shape, 2)
    zero = jnp.zeros_like(p[:1])
    px = jnp.where(row == nx - 1, 0.0, pltpu.roll(p, nx - 1, 1))
    py = jnp.where(lane == ny - 1, 0.0, pltpu.roll(p, ny - 1, 2))
    pz = jnp.concatenate([p[1:], zero], axis=0)
    vx = vx - h * (px - p)
    vy = vy - h * (py - p)
    vz = vz - h * (pz - p)
    bx = jnp.where(row == 0, 0.0, pltpu.roll(vx, 1, 1))
    by = jnp.where(lane == 0, 0.0, pltpu.roll(vy, 1, 2))
    bz = jnp.concatenate([zero, vz[:-1]], axis=0)
    p = p - h * speed_sq * ((vx - bx) + (vy - by) + (vz - bz))
    return (p, vx, vy, vz)


def make_kernel(n_tm, n_sp, rank, slab):
    n_chain = n_tm // GROUP - 1

    def kernel(
        speed_in, forcing_in, guess_in, basis_in, states_out, coords_out,
        speed, forcing, basis, rx, tx, ys, cf, gb, inv, acc, wb,
        local_sem, in_s, in_r, sh_s, sh_r, y_s, y_r, c_s, c_r, g_s, g_r,
    ):
        k = lax.axis_index("tm")
        s = lax.axis_index("space")
        nxt = lax.rem(k + 1, n_tm)
        mine = pl.ds(slab * s, slab)

        def peer(d):
            return lax.rem(s + d, n_sp)

        copies = [
            pltpu.make_async_copy(speed_in, speed.at[mine], local_sem.at[1]),
            pltpu.make_async_copy(forcing_in, forcing.at[:, mine], local_sem.at[2]),
            pltpu.make_async_copy(basis_in, basis, local_sem.at[3]),
        ]
        for c in copies:
            c.start()

        partners = [(k, peer(d)) for d in range(1, n_sp)]
        for d in range(n_sp):
            partners.append((nxt, peer(d)))
            partners.append((lax.rem(k + n_tm - 1, n_tm), peer(d)))
        for j in range(1, n_chain + 1):
            partners.append((lax.rem(k + 1 + GROUP * j, n_tm), s))
            partners.append((lax.rem(k + n_tm - 1 - GROUP * j, n_tm), s))
        barrier = pltpu.get_barrier_semaphore()
        for target in partners:
            pl.semaphore_signal(barrier, inc=1, device_id=target, device_id_type=MESH)
        pl.semaphore_wait(barrier, len(partners))

        def remote(src, dst, send, recv, target):
            c = pltpu.make_async_remote_copy(
                src_ref=src, dst_ref=dst, send_sem=send, recv_sem=recv,
                device_id=target, device_id_type=MESH,
            )
            c.start()
            return c

        sent = []
        first = []
        for d in range(n_sp):
            first.append(remote(guess_in, rx.at[0, :, mine], in_s.at[0, d], in_r.at[0, d], (nxt, peer(d))))
        for d in range(1, n_sp):
            first.append(remote(speed_in, speed.at[mine], in_s.at[1, d], in_r.at[1, d], (k, peer(d))))
            first.append(remote(forcing_in, forcing.at[:, mine], in_s.at[2, d], in_r.at[2, d], (k, peer(d))))
        sent += first

        def load(ref):
            return tuple(ref[i] for i in range(4))

        def store(ref, state):
            for i in range(4):
                ref[i] = state[i]

        def fine(i, state):
            p, vx, vy, vz = phi(state, speed[...] * speed[...], DT)
            return (p + forcing[i], vx, vy, vz)

        def plain(i, state):
            return phi(state, speed[...] * speed[...], DT)

        def shift_whole(index, src, hop):
            c = remote(src, rx.at[index], sh_s.at[index, 0], sh_r.at[index, 0], (lax.rem(k + hop, n_tm), s))
            sent.append(c)
            return c

        def shift_slabs(index, src):
            made = []
            for d in range(n_sp):
                part = pl.ds(slab * peer(d), slab)
                made.append(remote(src.at[:, part], rx.at[index, :, part], sh_s.at[index, d], sh_r.at[index, d], (nxt, s)))
            sent.extend(made)
            return made

        copies[2].wait()

        def gram_step(i, total):
            t = jnp.swapaxes(basis[:, i], 0, 1)
            hi = t.astype(jnp.bfloat16)
            rest = t - hi.astype(jnp.float32)
            mid = rest.astype(jnp.bfloat16)
            low = (rest - mid.astype(jnp.float32)).astype(jnp.bfloat16)
            parts = jnp.concatenate([hi, mid, low], axis=1)
            flat = jnp.concatenate([parts[j] for j in range(parts.shape[0])], axis=1)
            return total + lax.dot_general(
                flat, flat, (((1,), (1,)), ((), ())), preferred_element_type=jnp.float32
            )

        full = lax.fori_loop(0, basis.shape[1], gram_step, jnp.zeros((3 * rank, 3 * rank), jnp.float32))
        hh, hm, hl = full[:rank, :rank], full[:rank, rank:2 * rank], full[:rank, 2 * rank:]
        mh, mm, lh = full[rank:2 * rank, :rank], full[rank:2 * rank, rank:2 * rank], full[2 * rank:, :rank]
        gram = hh + ((hm + mh) + (mm + (hl + lh)))
        gb[s] = jnp.concatenate([gram, jnp.zeros_like(gram)], axis=1)
        gram_copies = [remote(gb.at[s], gb.at[s], g_s.at[d], g_r.at[d], (k, peer(d))) for d in range(1, n_sp)]
        sent += gram_copies

        copies[0].wait()
        copies[1].wait()
        for c in first:
            c.wait_recv()
        state = lax.fori_loop(0, 4, fine, load(rx.at[0]))
        store(tx.at[0], state)
        moved = shift_whole(1, tx.at[0], 1)

        for c in gram_copies:
            c.wait_recv()
        g = gb[0]
        for i in range(1, n_sp):
            g = g + gb[i]
        rows = lax.broadcasted_iota(jnp.int32, g.shape, 0)
        lanes = lax.broadcasted_iota(jnp.int32, g.shape, 1)
        m = jnp.where(lanes == rows + rank, 1.0, g)
        for j in range(rank):
            pivot = m[j:j + 1]
            pivot = pivot / pivot[:, j:j + 1]
            m = jnp.where(rows == j, pivot, m - m[:, j:j + 1] * pivot)
        inverse = m[:, rank:]
        inv[...] = jnp.concatenate([inverse, jnp.zeros_like(inverse)], axis=1)
        acc[rank:, :] = jnp.zeros((rank, acc.shape[1]), jnp.float32)

        moved.wait_recv()
        state = lax.fori_loop(0, 4, fine, load(rx.at[1]))
        residue = tx.at[1]
        for i in range(4):
            residue[i] = state[i] - tx[0, i]

        def weights(index, x):
            def coef_step(i, carry):
                b = basis[pl.ds(8 * i, 8)]
                t = jnp.sum(b * x[None], axis=1)
                half = t.shape[1] // 2
                t = t[:, :half] + t[:, half:]
                acc[pl.ds(pl.multiple_of(8 * i, 8), 8), :] = jnp.sum(t, axis=1)
                return carry

            lax.fori_loop(0, rank // 8, coef_step, 0)
            ones = jnp.ones((8, acc.shape[1]), jnp.float32)
            cf[index, s] = lax.dot_general(
                ones, acc[...], (((1,), (1,)), ((), ())),
                precision=lax.Precision.HIGHEST, preferred_element_type=jnp.float32,
            )
            made = [
                remote(cf.at[index, s], cf.at[index, s], c_s.at[index, d], c_r.at[index, d], (k, peer(d)))
                for d in range(1, n_sp)
            ]
            sent.extend(made)
            return made

        def solve(index, made):
            for c in made:
                c.wait_recv()
            total = cf[index, 0]
            for i in range(1, n_sp):
                total = total + cf[index, i]
            w = jnp.sum(inv[...] * total[:1], axis=1, keepdims=True)
            return jnp.broadcast_to(w, wb.shape)

        def slab_of(ref):
            x = ref[:, mine]
            return x.reshape((x.shape[0] * x.shape[1],) + x.shape[2:])

        def candidate(index, x_ref, late):
            wb[...] = solve(index, weights(index, slab_of(x_ref)))

            def sum_step(r, y):
                return y + wb[pl.ds(r, 1), :][None] * basis[r]

            y = lax.fori_loop(0, rank, sum_step, jnp.zeros(basis.shape[1:], jnp.float32), unroll=4)
            ys[index, :, mine] = y.reshape((4, slab) + y.shape[1:])
            made = [
                remote(ys.at[index, :, mine], ys.at[index, :, mine], y_s.at[index, d], y_r.at[index, d], (k, peer(d)))
                for d in range(1, n_sp)
            ]
            sent.extend(made)
            for c in late + made:
                c.wait_recv()
            ally = load(ys.at[index])
            ahead = phi(tuple(x_ref[i] - ally[i] for i in range(4)), speed[...] * speed[...], 4 * DT)
            for i in range(4):
                acc4[i] = ahead[i] + residue[i]
            corrected = lax.fori_loop(0, 4, plain, load(ys.at[index]))
            return tuple(corrected[i] + acc4[i] for i in range(4))

        acc4 = tx.at[6]

        moved = shift_slabs(2, residue)
        for index in range(3):
            moved[0].wait_recv()
            level = candidate(index, rx.at[2 + index], moved[1:])
            store(tx.at[2 + index], level)
            if index < 2:
                moved = shift_slabs(3 + index, tx.at[2 + index])
        for i in range(4):
            tx[5, i] = tx[4, i] - tx[3, i]
        chains = [shift_whole(6 + j, tx.at[5], 1 + GROUP * j) for j in range(1, n_chain + 1)]
        moved = shift_whole(5, tx.at[4], 1)
        source = lax.rem(k + n_tm - 1, n_tm)
        carry = None
        for j in range(n_chain, 0, -1):
            chains[j - 1].wait_recv()
            keep = (source >= GROUP * j).astype(jnp.float32)
            gap = tuple(keep * rx[6 + j, i] for i in range(4))
            carry = gap if carry is None else tuple(a + b for a, b in zip(gap, carry))
            carry = lax.fori_loop(0, 2, lambda i, u: phi(u, speed[...] * speed[...], 8 * DT), carry)
        moved.wait_recv()
        x_ref = rx.at[5]
        if carry is not None:
            for i in range(4):
                ys[4, i] = rx[5, i] + carry[i]
            x_ref = ys.at[4]
        level = candidate(3, x_ref, [])
        final = tx.at[7]
        for i in range(4):
            final[i] = tx[0, i] + level[i]
        moved = shift_whole(6, final, 1)
        made = weights(4, slab_of(final))
        states_out[3] = final[:, mine]
        w = solve(4, made)
        rows = lax.broadcasted_iota(jnp.int32, w.shape, 0)
        lanes = lax.broadcasted_iota(jnp.int32, w.shape, 1)
        coords_out[...] = jnp.sum(jnp.where(rows == lanes, w, 0.0), axis=0, keepdims=True)[:, :rank]
        moved.wait_recv()
        state = load(rx.at[6])
        for n in range(3):
            state = fine(n, state)
            store(acc4, state)
            states_out[n] = acc4[:, mine]
        for c in sent:
            c.wait_send()

    return kernel


def solution(mesh):
    n_tm, n_sp = mesh.shape["tm"], mesh.shape["space"]

    def body(speed, forcing, guess, basis):
        rank = basis.shape[1]
        slab, nx, ny = speed.shape
        nz = slab * n_sp
        n_chain = n_tm // GROUP - 1
        f32 = jnp.float32
        dma = pltpu.SemaphoreType.DMA
        return pl.pallas_call(
            make_kernel(n_tm, n_sp, rank, slab),
            out_shape=(
                jax.ShapeDtypeStruct((4, 4, slab, nx, ny), f32),
                jax.ShapeDtypeStruct((1, rank), f32),
            ),
            in_specs=[pl.BlockSpec(memory_space=pl.ANY)] * 4,
            out_specs=(pl.BlockSpec(memory_space=pltpu.VMEM),) * 2,
            scratch_shapes=[
                pltpu.VMEM((nz, nx, ny), f32),
                pltpu.VMEM((4, nz, nx, ny), f32),
                pltpu.VMEM((rank, 4 * slab, nx, ny), f32),
                pltpu.VMEM((7 + n_chain, 4, nz, nx, ny), f32),
                pltpu.VMEM((8, 4, nz, nx, ny), f32),
                pltpu.VMEM((5, 4, nz, nx, ny), f32),
                pltpu.VMEM((5, n_sp, 8, 2 * rank), f32),
                pltpu.VMEM((n_sp, rank, 2 * rank), f32),
                pltpu.VMEM((rank, 2 * rank), f32),
                pltpu.VMEM((2 * rank, ny), f32),
                pltpu.VMEM((rank, ny), f32),
                dma((4,)),
                dma((3, n_sp)), dma((3, n_sp)),
                dma((7 + n_chain, n_sp)), dma((7 + n_chain, n_sp)),
                dma((4, n_sp)), dma((4, n_sp)),
                dma((5, n_sp)), dma((5, n_sp)),
                dma((n_sp,)), dma((n_sp,)),
            ],
            compiler_params=pltpu.CompilerParams(
                collective_id=0, has_side_effects=True, vmem_limit_bytes=48 * 1024 * 1024
            ),
        )(speed, forcing, guess[0], basis[0].reshape(rank, 4 * slab, nx, ny))

    placed = (
        P("space", None, None),
        P("tm", "space", None, None),
        P("tm", None, "space", None, None),
        P("tm", None, None, "space", None, None),
    )
    return jax.shard_map(
        body,
        mesh=mesh,
        in_specs=placed,
        out_specs=(P("tm", None, "space", None, None), P("tm", None)),
        check_vma=False,
    )
```

profile of v0, /device:TPU:1, one launch (start us, length us, event | category | flops | bytes accessed | tf_op | source)
XLA Modules:
  0.0 102.5 jit_solution(13077771973433358964)
XLA Ops:
  0.6 0.0 copy-start
  0.6 2.2 %copy-done = f32[1,64,4,2,16,128]{5,4,3,2,1,0:T(8,128)S(1)} copy-done((f32[1,64,4,2,16,128]{5,4,3,2,1,0:T(8,128)S(1)}, f32[1,64,4,2,16,128]{5,4,3,2,1,0:T(8,128)}, u32[]{:S(2)}) %copy-start) | copy-done | bytes 4194328
  2.8 0.0 copy-start.1
  2.8 0.8 copy-done.1
  3.7 0.0 copy-start.2
  3.7 0.8 copy-done.2
  4.5 0.0 copy-start.3
  4.5 0.7 copy-done.3
  5.2 96.0 %shard_map.59 = (f32[4,4,2,16,128]{4,3,2,1,0:T(8,128)S(1)}, f32[1,64]{1,0:T(1,128)S(1)}) custom-call(f32[2,16,128]{2,1,0:T(8,128)S(1)} %copy-done.3, f32[4,2,16,128]{3,2,1,0:T(8,128)S(1)} %copy-done.1, f32[4,2,16,128]{3,2,1,0:T(8,128)S(1)} %bitcast.3, f32[64,8,16,128]{3,2,1,0:T(8,128)S(1)} %bitcast.2), custom_call_target="tpu_custom_call" | custom-call | tf_op jit(solution)/shard_map/pallas_call | solution.py:281
  101.3 0.7 copy.8
  102.0 0.5 copy.9
Async XLA Ops:
  0.6 2.2 %copy-start = (f32[1,64,4,2,16,128]{5,4,3,2,1,0:T(8,128)S(1)}, f32[1,64,4,2,16,128]{5,4,3,2,1,0:T(8,128)}, u32[]{:S(2)}) copy-start(f32[1,64,4,2,16,128]{5,4,3,2,1,0:T(8,128)} %param.7) | copy-start | bytes 12582916
  2.8 0.8 copy-start.1
  3.7 0.8 copy-start.2
  4.5 0.7 copy-start.3
where the time goes:
time: 103 us; the launch traced here: 102 us
  Pallas kernels  96 us (93%)
  local copies, waits for them, and re-layouts  5.79 us (6%)
    pallas_call x1, Pallas kernels, body(): pl.pallas_call(make_kernel(n_tm, n_sp, rank, slab), out_shape=(jax.ShapeD...  96 us
    unnamed x10, local copies, waits for them, and re-layouts  5.79 us

commit v1 on v0

--- a/solution.py
+++ b/solution.py
@@ -35,7 +35,7 @@
     def kernel(
         speed_in, forcing_in, guess_in, basis_in, states_out, coords_out,
         speed, forcing, basis, rx, tx, ys, cf, gb, inv, acc, wb,
-        local_sem, in_s, in_r, sh_s, sh_r, y_s, y_r, c_s, c_r, g_s, g_r,
+        local_sem, send_sems, recv_sems,
     ):
         k = lax.axis_index("tm")
         s = lax.axis_index("space")
@@ -46,41 +46,101 @@
             return lax.rem(s + d, n_sp)
 
         copies = [
-            pltpu.make_async_copy(speed_in, speed.at[mine], local_sem.at[1]),
+            pltpu.make_async_copy(speed_in, speed.at[:, mine], local_sem.at[1]),
             pltpu.make_async_copy(forcing_in, forcing.at[:, mine], local_sem.at[2]),
             pltpu.make_async_copy(basis_in, basis, local_sem.at[3]),
         ]
         for c in copies:
             c.start()
 
+        before = lax.rem(k + n_tm - 1, n_tm)
         partners = [(k, peer(d)) for d in range(1, n_sp)]
-        for d in range(n_sp):
-            partners.append((nxt, peer(d)))
-            partners.append((lax.rem(k + n_tm - 1, n_tm), peer(d)))
+        groups = [nxt, before]
         for j in range(1, n_chain + 1):
-            partners.append((lax.rem(k + 1 + GROUP * j, n_tm), s))
-            partners.append((lax.rem(k + n_tm - 1 - GROUP * j, n_tm), s))
+            groups.append(lax.rem(k + 1 + GROUP * j, n_tm))
+            groups.append(lax.rem(k + n_tm - 1 - GROUP * j, n_tm))
+        for group in groups:
+            partners += [(group, peer(d)) for d in range(n_sp)]
         barrier = pltpu.get_barrier_semaphore()
         for target in partners:
             pl.semaphore_signal(barrier, inc=1, device_id=target, device_id_type=MESH)
         pl.semaphore_wait(barrier, len(partners))
 
-        def remote(src, dst, send, recv, target):
-            c = pltpu.make_async_remote_copy(
-                src_ref=src, dst_ref=dst, send_sem=send, recv_sem=recv,
-                device_id=target, device_id_type=MESH,
-            )
-            c.start()
-            return c
-
         sent = []
-        first = []
-        for d in range(n_sp):
-            first.append(remote(guess_in, rx.at[0, :, mine], in_s.at[0, d], in_r.at[0, d], (nxt, peer(d))))
-        for d in range(1, n_sp):
-            first.append(remote(speed_in, speed.at[mine], in_s.at[1, d], in_r.at[1, d], (k, peer(d))))
-            first.append(remote(forcing_in, forcing.at[:, mine], in_s.at[2, d], in_r.at[2, d], (k, peer(d))))
-        sent += first
+
+        class Remote:
+            def __init__(self, src, dst, target, sends=None, receives=None):
+                i = len(sent)
+                self.copy = pltpu.make_async_remote_copy(
+                    src_ref=src, dst_ref=dst, send_sem=send_sems.at[i], recv_sem=recv_sems.at[i],
+                    device_id=target, device_id_type=MESH,
+                )
+                self.sends, self.receives = sends, receives
+                sent.append(self)
+                self.under(sends, self.copy.start)
+
+            def under(self, condition, act):
+                if condition is None:
+                    act()
+                else:
+                    pl.when(condition)(act)
+
+            def wait_recv(self):
+                self.under(self.receives, self.copy.wait_recv)
+
+            def wait_send(self):
+                self.under(self.sends, self.copy.wait_send)
+
+        def remote(src, dst, target):
+            return Remote(src, dst, target)
+
+        def inside(at):
+            return (at >= 0) & (at < n_sp)
+
+        def spread(src, base, dst, group, pieces):
+            made = []
+            for delta, comps, offset, planes in pieces:
+                made.append(Remote(
+                    src.at[comps, pl.ds(base + offset, planes)],
+                    dst.at[comps, pl.ds(slab * s + offset, planes)],
+                    (group, s + delta),
+                    None if delta == 0 else inside(s + delta),
+                    None if delta == 0 else inside(s - delta),
+                ))
+            return made
+
+        def state_pieces(reach):
+            pieces = []
+            delta = 1
+            while reach - (delta - 1) * slab > 0:
+                left = reach - (delta - 1) * slab
+                near = min(slab, left - 1)
+                if near:
+                    pieces.append((delta, slice(0, 4), slab - near, near))
+                    pieces.append((-delta, slice(0, 4), 0, near))
+                if left <= slab:
+                    pieces.append((delta, slice(0, 1), slab - left, 1))
+                    pieces.append((delta, slice(3, 4), slab - left, 1))
+                    pieces.append((-delta, slice(0, 1), left - 1, 1))
+                delta += 1
+            return pieces
+
+        own = [(0, slice(0, 4), 0, slab)]
+
+        def load_pieces(reach):
+            pieces = []
+            delta = 1
+            while reach - (delta - 1) * slab > 0:
+                left = reach - (delta - 1) * slab
+                planes = min(slab, left)
+                pieces.append((delta, slice(0, left), slab - planes, planes))
+                pieces.append((-delta, slice(0, left), 0, planes))
+                delta += 1
+            return pieces
+
+        first = spread(guess_in, 0, rx.at[0], nxt, own + state_pieces(4))
+        first += spread(forcing_in, 0, forcing, k, load_pieces(3))
+        first += spread(speed_in, 0, speed, k, [(d, slice(0, 1), o, n) for d, c, o, n in load_pieces(3)])
 
         def load(ref):
             return tuple(ref[i] for i in range(4))
@@ -90,24 +150,14 @@
                 ref[i] = state[i]
 
         def fine(i, state):
-            p, vx, vy, vz = phi(state, speed[...] * speed[...], DT)
+            p, vx, vy, vz = phi(state, speed[0] * speed[0], DT)
             return (p + forcing[i], vx, vy, vz)
 
         def plain(i, state):
-            return phi(state, speed[...] * speed[...], DT)
-
-        def shift_whole(index, src, hop):
-            c = remote(src, rx.at[index], sh_s.at[index, 0], sh_r.at[index, 0], (lax.rem(k + hop, n_tm), s))
-            sent.append(c)
-            return c
-
-        def shift_slabs(index, src):
-            made = []
-            for d in range(n_sp):
-                part = pl.ds(slab * peer(d), slab)
-                made.append(remote(src.at[:, part], rx.at[index, :, part], sh_s.at[index, d], sh_r.at[index, d], (nxt, s)))
-            sent.extend(made)
-            return made
+            return phi(state, speed[0] * speed[0], DT)
+
+        def shift(index, src, group, reach):
+            return spread(src, slab * s, rx.at[index], group, own + state_pieces(reach))
 
         copies[2].wait()
 
@@ -128,8 +178,7 @@
         mh, mm, lh = full[rank:2 * rank, :rank], full[rank:2 * rank, rank:2 * rank], full[2 * rank:, :rank]
         gram = hh + ((hm + mh) + (mm + (hl + lh)))
         gb[s] = jnp.concatenate([gram, jnp.zeros_like(gram)], axis=1)
-        gram_copies = [remote(gb.at[s], gb.at[s], g_s.at[d], g_r.at[d], (k, peer(d))) for d in range(1, n_sp)]
-        sent += gram_copies
+        gram_copies = [remote(gb.at[s], gb.at[s], (k, peer(d))) for d in range(1, n_sp)]
 
         copies[0].wait()
         copies[1].wait()
@@ -137,7 +186,7 @@
             c.wait_recv()
         state = lax.fori_loop(0, 4, fine, load(rx.at[0]))
         store(tx.at[0], state)
-        moved = shift_whole(1, tx.at[0], 1)
+        moved = shift(1, tx.at[0], nxt, 4)
 
         for c in gram_copies:
             c.wait_recv()
@@ -155,7 +204,8 @@
         inv[...] = jnp.concatenate([inverse, jnp.zeros_like(inverse)], axis=1)
         acc[rank:, :] = jnp.zeros((rank, acc.shape[1]), jnp.float32)
 
-        moved.wait_recv()
+        for c in moved:
+            c.wait_recv()
         state = lax.fori_loop(0, 4, fine, load(rx.at[1]))
         residue = tx.at[1]
         for i in range(4):
@@ -177,10 +227,9 @@
                 precision=lax.Precision.HIGHEST, preferred_element_type=jnp.float32,
             )
             made = [
-                remote(cf.at[index, s], cf.at[index, s], c_s.at[index, d], c_r.at[index, d], (k, peer(d)))
+                remote(cf.at[index, s], cf.at[index, s], (k, peer(d)))
                 for d in range(1, n_sp)
             ]
-            sent.extend(made)
             return made
 
         def solve(index, made):
@@ -204,15 +253,11 @@
 
             y = lax.fori_loop(0, rank, sum_step, jnp.zeros(basis.shape[1:], jnp.float32), unroll=4)
             ys[index, :, mine] = y.reshape((4, slab) + y.shape[1:])
-            made = [
-                remote(ys.at[index, :, mine], ys.at[index, :, mine], y_s.at[index, d], y_r.at[index, d], (k, peer(d)))
-                for d in range(1, n_sp)
-            ]
-            sent.extend(made)
+            made = spread(ys.at[index], slab * s, ys.at[index], k, state_pieces(4))
             for c in late + made:
                 c.wait_recv()
             ally = load(ys.at[index])
-            ahead = phi(tuple(x_ref[i] - ally[i] for i in range(4)), speed[...] * speed[...], 4 * DT)
+            ahead = phi(tuple(x_ref[i] - ally[i] for i in range(4)), speed[0] * speed[0], 4 * DT)
             for i in range(4):
                 acc4[i] = ahead[i] + residue[i]
             corrected = lax.fori_loop(0, 4, plain, load(ys.at[index]))
@@ -220,26 +265,26 @@
 
         acc4 = tx.at[6]
 
-        moved = shift_slabs(2, residue)
+        moved = shift(2, residue, nxt, 1)
         for index in range(3):
             moved[0].wait_recv()
             level = candidate(index, rx.at[2 + index], moved[1:])
             store(tx.at[2 + index], level)
             if index < 2:
-                moved = shift_slabs(3 + index, tx.at[2 + index])
+                moved = shift(3 + index, tx.at[2 + index], nxt, 1)
         for i in range(4):
             tx[5, i] = tx[4, i] - tx[3, i]
-        chains = [shift_whole(6 + j, tx.at[5], 1 + GROUP * j) for j in range(1, n_chain + 1)]
-        moved = shift_whole(5, tx.at[4], 1)
-        source = lax.rem(k + n_tm - 1, n_tm)
+        chains = [shift(6 + j, tx.at[5], lax.rem(k + 1 + GROUP * j, n_tm), 2 * j + 1) for j in range(1, n_chain + 1)]
+        moved = shift(5, tx.at[4], nxt, 1)
         carry = None
         for j in range(n_chain, 0, -1):
-            chains[j - 1].wait_recv()
-            keep = (source >= GROUP * j).astype(jnp.float32)
-            gap = tuple(keep * rx[6 + j, i] for i in range(4))
+            for c in chains[j - 1]:
+                c.wait_recv()
+            gap = tuple(jnp.where(before >= GROUP * j, rx[6 + j, i], 0.0) for i in range(4))
             carry = gap if carry is None else tuple(a + b for a, b in zip(gap, carry))
-            carry = lax.fori_loop(0, 2, lambda i, u: phi(u, speed[...] * speed[...], 8 * DT), carry)
-        moved.wait_recv()
+            carry = lax.fori_loop(0, 2, lambda i, u: phi(u, speed[0] * speed[0], 8 * DT), carry)
+        for c in moved:
+            c.wait_recv()
         x_ref = rx.at[5]
         if carry is not None:
             for i in range(4):
@@ -249,14 +294,15 @@
         final = tx.at[7]
         for i in range(4):
             final[i] = tx[0, i] + level[i]
-        moved = shift_whole(6, final, 1)
+        moved = shift(6, final, nxt, 3)
         made = weights(4, slab_of(final))
         states_out[3] = final[:, mine]
         w = solve(4, made)
         rows = lax.broadcasted_iota(jnp.int32, w.shape, 0)
         lanes = lax.broadcasted_iota(jnp.int32, w.shape, 1)
         coords_out[...] = jnp.sum(jnp.where(rows == lanes, w, 0.0), axis=0, keepdims=True)[:, :rank]
-        moved.wait_recv()
+        for c in moved:
+            c.wait_recv()
         state = load(rx.at[6])
         for n in range(3):
             state = fine(n, state)
@@ -287,7 +333,7 @@
             in_specs=[pl.BlockSpec(memory_space=pl.ANY)] * 4,
             out_specs=(pl.BlockSpec(memory_space=pltpu.VMEM),) * 2,
             scratch_shapes=[
-                pltpu.VMEM((nz, nx, ny), f32),
+                pltpu.VMEM((1, nz, nx, ny), f32),
                 pltpu.VMEM((4, nz, nx, ny), f32),
                 pltpu.VMEM((rank, 4 * slab, nx, ny), f32),
                 pltpu.VMEM((7 + n_chain, 4, nz, nx, ny), f32),
@@ -299,16 +345,12 @@
                 pltpu.VMEM((2 * rank, ny), f32),
                 pltpu.VMEM((rank, ny), f32),
                 dma((4,)),
-                dma((3, n_sp)), dma((3, n_sp)),
-                dma((7 + n_chain, n_sp)), dma((7 + n_chain, n_sp)),
-                dma((4, n_sp)), dma((4, n_sp)),
-                dma((5, n_sp)), dma((5, n_sp)),
-                dma((n_sp,)), dma((n_sp,)),
+                dma((128 + 6 * n_sp,)), dma((128 + 6 * n_sp,)),
             ],
             compiler_params=pltpu.CompilerParams(
-                collective_id=0, has_side_effects=True, vmem_limit_bytes=48 * 1024 * 1024
+                collective_id=0, has_side_effects=True, vmem_limit_bytes=60 * 1024 * 1024
             ),
-        )(speed, forcing, guess[0], basis[0].reshape(rank, 4 * slab, nx, ny))
+        )(speed[None], forcing, guess[0], basis[0].reshape(rank, 4 * slab, nx, ny))
 
     placed = (
         P("space", None, None),

time: 103 us -> 85.2 us (0.83)
  Pallas kernels: 96 us -> 81.3 us
  local copies, waits for them, and re-layouts: 5.79 us -> 2.8 us
    pallas_call x1, Pallas kernels: 96 us -> 81.3 us  [body(): pl.pallas_call(make_kernel(n_tm, n_sp, rank, slab), out_shape=(jax.ShapeD...]
    unnamed x10 -> x2, local copies, waits for them, and re-layouts: 5.79 us -> 2.8 us
where the time goes in v1:
time: 85.2 us; the launch traced here: 84.7 us
  Pallas kernels  81.3 us (95%)
  local copies, waits for them, and re-layouts  2.8 us (3%)
    pallas_call x1, Pallas kernels, body(): pl.pallas_call(make_kernel(n_tm, n_sp, rank, slab), out_shape=(jax.ShapeD...  81.3 us
    unnamed x2, local copies, waits for them, and re-layouts  2.8 us

profile of v1, /device:TPU:1, one launch (start us, length us, event | category | flops | bytes accessed | tf_op | source)
XLA Modules:
  0.0 84.7 jit_solution(16372506939324837290)
XLA Ops:
  0.6 81.3 %shard_map.59 = (f32[4,4,2,16,128]{4,3,2,1,0:T(8,128)}, f32[1,64]{1,0:T(1,128)}) custom-call(f32[1,2,16,128]{3,2,1,0:T(8,128)} %bitcast.5, f32[4,2,16,128]{3,2,1,0:T(8,128)} %forcing_in.1, f32[4,2,16,128]{3,2,1,0:T(8,128)} %bitcast.4, f32[64,8,16,128]{3,2,1,0:T(8,128)} %bitcast.3), custom_call_target="tpu_custom_call" | custom-call | tf_op jit(solution)/shard_map/pallas_call | solution.py:327
  81.9 1.7 %copy.8 = f32[4,4,2,16,128]{4,3,2,1,0:T(8,128)} copy(f32[4,4,2,16,128]{4,3,2,1,0:T(8,128)} %get-tuple-element.4) | data formatting | bytes 524288
  83.6 1.1 %copy.9 = f32[1,64]{1,0:T(1,128)} copy(f32[1,64]{1,0:T(1,128)} %get-tuple-element.5) | data formatting | bytes 512
